TPU v7x, 32 devices: a whole 2x2x4 slice. The times are simulated.
32 devices in a mesh: head: 2 (over y), seq: 16 (over z, x, core).
Axes of the slice: x: 2, y: 2, z: 4, core: 2. Of those that a mesh axis runs over, the one named last changes fastest.
Arguments:
- queries: bfloat16 [2048, 4096], P(('seq', 'head')), may hold values from -20 to 20
- keys: bfloat16 [2048, 1024], P(('seq', 'head')), may hold values from -5 to 5
- values: bfloat16 [2048, 1024], P(('seq', 'head')), may hold values from -6 to 6
Outputs:
- attended: bfloat16 [2048, 4096], P(('seq', 'head'))
All inputs are finite; a program needn't handle non-finite values.
Results may differ from a plain program's by a relative error of at most 0.0041.
Values may be sent and summed in bfloat16 or wider, within the bound.
No kernel may reach another device: no remote copies, remote signals or barrier semaphores. Data moves between devices by JAX's collectives and lax.ppermute only.
A program may use at most 64 MiB of HBM per device.

v0:
```python
import math
import jax
import jax.numpy as jnp
from jax import lax
from jax.sharding import PartitionSpec as P

HEAD_DIM = 128


def update_state(state, query_half, query_pos, key_piece, value_piece, key_pos):
    largest, total, summed = state
    score = jnp.einsum("tkgd,pkd->tkgp", query_half, key_piece, preferred_element_type=jnp.float32)
    score = score / math.sqrt(query_half.shape[-1])
    allowed = (key_pos[None, :] <= query_pos[:, None])[:, None, None, :]
    score = jnp.where(allowed, score, jnp.float32(-1e30))
    new_largest = jnp.maximum(largest, jnp.max(score, axis=-1))
    weight = jnp.where(allowed, jnp.exp(score - new_largest[..., None]), jnp.float32(0.0))
    total = jnp.sum(weight, axis=-1)
    product = jnp.einsum(
        "tkgp,pkd->tkgd",
        weight.astype(jnp.bfloat16),
        value_piece,
        preferred_element_type=jnp.float32,
    )
    summed = product
    return (new_largest, total, summed)


def on_device(queries, keys, values):
    q_local, k_local, v_local = (
        lax.all_to_all(queries, "head", split_axis=1, concat_axis=0, tiled=True),
        lax.all_to_all(keys, "head", split_axis=1, concat_axis=0, tiled=True),
        lax.all_to_all(values, "head", split_axis=1, concat_axis=0, tiled=True),
    )
    tokens = q_local.shape[0]
    half = tokens // 2
    kv_local = k_local.shape[1] // HEAD_DIM
    group = q_local.shape[1] // k_local.shape[1]
    index = lax.axis_index("seq")
    offsets = jnp.arange(half, dtype=jnp.int32)
    later = q_local[half:]
    early_pos = index * tokens + offsets
    later_pos = index * tokens + half + offsets
    query_pos = jnp.stack([early_pos, later_pos])
    halves = jnp.stack([q_local[:half], later]).reshape(2, half, kv_local, group, HEAD_DIM)
    start_state = (
        jnp.full((2, half, kv_local, group), -1e30, jnp.float32),
        jnp.zeros((2, half, kv_local, group), jnp.float32),
        jnp.zeros((2, half, kv_local, group, HEAD_DIM), jnp.float32),
    )
    start = jnp.int32(0)
    key_piece = lax.all_gather(k_local, "seq", axis=0, tiled=True)
    value_piece = lax.all_gather(v_local, "seq", axis=0, tiled=True)
    rows = key_piece.shape[0]
    key_piece = key_piece.reshape(rows, kv_local, HEAD_DIM)
    value_piece = value_piece.reshape(rows, kv_local, HEAD_DIM)
    key_pos = jnp.arange(rows, dtype=jnp.int32)
    results = []
    for which in range(2):
        state = (start_state[0][which], start_state[1][which], start_state[2][which])
        needed = start <= query_pos[which, half - 1]

        def run(current, which=which):
            return update_state(
                current, halves[which], query_pos[which], key_piece, value_piece, key_pos
            )

        def keep(current):
            return current

        results.append(lax.cond(needed, run, keep, state))
    total = jnp.stack([results[0][1], results[1][1]])
    summed = jnp.stack([results[0][2], results[1][2]])
    result = (summed / total[..., None]).reshape(2, half, q_local.shape[1]).astype(jnp.bfloat16)
    later_out = result[1]
    combined = jnp.concatenate([result[0], later_out], axis=0)
    return lax.all_to_all(combined, "head", split_axis=0, concat_axis=1, tiled=True)


def solution(mesh):
    return jax.shard_map(
        on_device,
        mesh=mesh,
        in_specs=(P(("seq", "head"), None), P(("seq", "head"), None), P(("seq", "head"), None)),
        out_specs=P(("seq", "head"), None),
        check_vma=False,
    )
```

profile of v0, /device:TPU:0, one launch (start us, length us, event | category | flops | bytes accessed | tf_op | source)
XLA Modules:
  0.0 142.9 jit_solution(106555980706747682)
XLA Ops:
  6.5 0.9 copy.81
  7.5 8.6 %all_to_all.73 = bf16[64,2,512]{2,0,1:T(8,128)(2,1)} all-to-all(bf16[64,2,512]{2,0,1:T(8,128)(2,1)S(1)} %bitcast.111), channel_id=1, replica_groups=mesh['head'=2,'seq'=16] {'head'}, dimensions={1} | all-to-all | bytes 262144 | tf_op jit(solution)/shard_map/all_to_all | solution.py:32
  16.2 0.9 copy.80
  17.1 7.5 %all_to_all.74 = bf16[64,2,512]{2,0,1:T(8,128)(2,1)} all-to-all(bf16[64,2,512]{2,0,1:T(8,128)(2,1)S(1)} %bitcast.112), channel_id=1, replica_groups=mesh['head'=2,'seq'=16] {'head'}, dimensions={1} | all-to-all | bytes 262144 | tf_op jit(solution)/shard_map/all_to_all | solution.py:33
  24.6 1.9 %copy.79 = bf16[8,2,8,2048]{3,2,0,1:T(8,128)(2,1)} copy(bf16[8,2,8,2048]{3,2,1,0:T(8,128)(2,1)} %bitcast.108) | data formatting | bytes 1048576 | tf_op jit(solution)/shard_map/all_to_all | solution.py:31
  26.5 3.5 %all-to-all-start = ((bf16[64,2,2048]{2,0,1:T(8,128)(2,1)}), bf16[64,2,2048]{2,0,1:T(8,128)(2,1)S(1)}, u32[]{:S(2)}, u32[]{:S(2)}) async-start(bf16[64,2,2048]{2,0,1:T(8,128)(2,1)} %bitcast.98), calls=%async_computation | async-start | bytes 1048576 | tf_op jit(solution)/shard_map/all_to_all | solution.py:31
  32.6 4.0 %all-to-all-done = bf16[64,2,2048]{2,0,1:T(8,128)(2,1)S(1)} async-done(((bf16[64,2,2048]{2,0,1:T(8,128)(2,1)}), bf16[64,2,2048]{2,0,1:T(8,128)(2,1)S(1)}, u32[]{:S(2)}, u32[]{:S(2)}) %all-to-all-start) | async-done | bytes 524320 | tf_op jit(solution)/shard_map/all_to_all | solution.py:31
  37.2 21.2 %all-gather.3.cloned.1.call-done = bf16[2048,512]{1,0:T(8,128)(2,1)} async-done(((bf16[128,512]{1,0:T(8,128)(2,1)}), bf16[2048,512]{1,0:T(8,128)(2,1)}) %all-gather.3.cloned.1.call-update) | async-done | bytes 2097168 | tf_op jit(solution)/shard_map/all_gather | solution.py:52
  58.4 2.9 %copy.49 = bf16[2048,512]{0,1:T(8,128)(2,1)S(1)} copy(bf16[2048,512]{1,0:T(8,128)(2,1)} %all-gather.3.cloned.1.call-done) | data formatting | bytes 4194304 | tf_op jit(solution)/shard_map/all_gather | solution.py:52
  61.3 39.4 %all-gather.5.cloned.1.call-done = bf16[2048,512]{1,0:T(8,128)(2,1)} async-done(((bf16[128,512]{1,0:T(8,128)(2,1)}), bf16[2048,512]{1,0:T(8,128)(2,1)}) %all-gather.5.cloned.1.call-update) | async-done | bytes 2097168 | tf_op jit(solution)/shard_map/all_gather | solution.py:53
  100.7 4.0 %copy.51 = bf16[2048,512]{0,1:T(8,128)(2,1)} copy(bf16[2048,512]{1,0:T(8,128)(2,1)} %all-gather.5.cloned.1.call-done) | data formatting | bytes 4194304 | tf_op jit(solution)/shard_map/all_gather | solution.py:53
  104.7 8.9 %conditional.2 = (f32[1,64,4,4]{1,3,2,0:T(4,128)S(1)}, f32[1,64,2048]{2,1,0:T(8,128)S(1)}) conditional(s32[]{:T(128)} %bitcast.12, () %tuple.29, (s32[2048]{0:T(1024)S(1)}, s32[]{:T(128)}, s32[64]{0:T(128)S(1)}, bf16[2,64,4,4,128]{4,3,2,1,0:T(4,128)(2,1)S(1)}, bf16[2048,4,128]{0,2,1:T(8,128)(2,1)S(1)}, ...), branch_computations={%region_0.0_spmd, %region_1.4_spmd} | conditional | flops 1101134848 | bytes 42238768 | solution.py:71
  105.1 1.7 %fusion = (f32[64,4,4]{0,2,1:T(4,128)S(1)}, f32[4,2048,64,4]{1,2,3,0:T(8,128)S(1)}) fusion(pred[64,2048]{1,0:T(8,128)(4,1)S(1)} %broadcast_compare_fusion, bf16[2,64,4,4,128]{4,1,3,2,0:T(8,128)(2,1)S(1)} %copy.52, bf16[2048,4,128]{0,2,1:T(8,128)(2,1)S(1)} %get-tuple-element.97), kind=kOutput, calls=%fused_computation.2 | convolution fusion | flops 543161344 | bytes 10883072 | tf_op jit(solution)/shard_map/cond/branch_1_fun/tkgd,pkd->tkgp/dot_general | solution.py:12
  106.8 1.9 %fusion.9 = f32[64,4,4,128]{3,0,2,1:T(8,128)S(1)} fusion(bf16[2048,4,128]{0,2,1:T(8,128)(2,1)S(1)} %copy-done, f32[4,2048,64,4]{1,2,3,0:T(8,128)S(1)} %get-tuple-element.106, f32[64,4,4]{0,2,1:T(4,128)S(1)} %broadcast_maximum_fusion, pred[64,2048]{1,0:T(8,128)(4,1)S(1)} %broadcast_compare_fusion), kind=kOutput, calls=%fused_computation.10 | convolution fusion | flops 547356672 | bytes 11145216 | tf_op jit(solution)/shard_map/cond/branch_1_fun/tkgp,pkd->tkgd/dot_general | solution.py:19
  108.7 2.5 %fusion.2 = f32[64,4,4]{0,2,1:T(4,128)S(1)} fusion(f32[4,2048,64,4]{1,2,3,0:T(8,128)S(1)} %get-tuple-element.106, f32[64,4,4]{0,2,1:T(4,128)S(1)} %broadcast_maximum_fusion, pred[64,2048]{1,0:T(8,128)(4,1)S(1)} %broadcast_compare_fusion), kind=kLoop, calls=%fused_computation.4 | loop fusion | flops 10484736 | bytes 8527872 | tf_op jit(solution)/shard_map/cond/branch_1_fun/reduce_sum | solution.py:18
  111.2 1.1 copy.45
  112.4 1.3 stack.31
  113.6 8.0 %conditional.3 = (f32[1,64,4,4]{1,3,2,0:T(4,128)S(1)}, f32[1,64,2048]{2,1,0:T(8,128)}) conditional(s32[]{:T(128)} %bitcast.20, () %tuple.31, (s32[2048]{0:T(1024)S(1)}, s32[]{:T(128)}, s32[64]{0:T(128)S(1)}, bf16[2,64,4,4,128]{4,3,2,1,0:T(4,128)(2,1)S(1)}, bf16[2048,4,128]{0,2,1:T(8,128)(2,1)S(1)}, /*index=5*/bf16[2048,4,128]{0,2,1:T(8,128)(2,1)}) %tuple.56), branch_computations={%region_4.5_spmd, %region_5.8_spmd} | conditional | flops 1101134848 | bytes 42238768 | solution.py:71
  114.1 1.7 %fusion.17 = (f32[64,4,4]{0,2,1:T(4,128)S(1)}, f32[4,2048,64,4]{1,2,3,0:T(8,128)S(1)}) fusion(pred[64,2048]{1,0:T(8,128)(4,1)S(1)} %broadcast_compare_fusion.1, bf16[2,64,4,4,128]{4,1,3,2,0:T(8,128)(2,1)S(1)} %copy.55, bf16[2048,4,128]{0,2,1:T(8,128)(2,1)S(1)} %get-tuple-element.103), kind=kOutput, calls=%fused_computation.20 | convolution fusion | flops 543161344 | bytes 10883072 | tf_op jit(solution)/shard_map/cond/branch_1_fun/tkgd,pkd->tkgp/dot_general | solution.py:12
  115.8 1.9 %fusion.26 = f32[64,4,4,128]{3,0,2,1:T(8,128)S(1)} fusion(bf16[2048,4,128]{0,2,1:T(8,128)(2,1)S(1)} %copy-done.1, f32[4,2048,64,4]{1,2,3,0:T(8,128)S(1)} %get-tuple-element.108, f32[64,4,4]{0,2,1:T(4,128)S(1)} %broadcast_maximum_fusion.1, pred[64,2048]{1,0:T(8,128)(4,1)S(1)} %broadcast_compare_fusion.1), kind=kOutput, calls=%fused_computation.28 | convolution fusion | flops 547356672 | bytes 11145216 | tf_op jit(solution)/shard_map/cond/branch_1_fun/tkgp,pkd->tkgd/dot_general | solution.py:19
  117.8 2.5 %fusion.19 = f32[64,4,4]{0,2,1:T(4,128)S(1)} fusion(f32[4,2048,64,4]{1,2,3,0:T(8,128)S(1)} %get-tuple-element.108, f32[64,4,4]{0,2,1:T(4,128)S(1)} %broadcast_maximum_fusion.1, pred[64,2048]{1,0:T(8,128)(4,1)S(1)} %broadcast_compare_fusion.1), kind=kLoop, calls=%fused_computation.22 | loop fusion | flops 10484736 | bytes 8527872 | tf_op jit(solution)/shard_map/cond/branch_1_fun/reduce_sum | solution.py:18
  120.7 1.0 stack.35
  122.9 1.2 fusion.34
  124.2 11.1 %all_to_all.75 = bf16[2,64,2048]{2,1,0:T(8,128)(2,1)S(1)} all-to-all(bf16[2,64,2048]{2,1,0:T(8,128)(2,1)S(1)} %bitcast.106), channel_id=1, replica_groups=mesh['head'=2,'seq'=16] {'head'}, dimensions={0} | all-to-all | bytes 1048576 | tf_op jit(solution)/shard_map/all_to_all | solution.py:77
  (37 shorter events, 5.0 us)
Async XLA Ops:
  6.5 51.8 %all-gather.3.cloned.1.call-start = ((), (), s32[]{:S(2)}) async-start(), calls=%async_computation.4 | async-start | bytes 2228224 | tf_op jit(solution)/shard_map/all_gather | solution.py:52
  16.1 84.6 %all-gather.5.cloned.1.call-start = ((), (), s32[]{:S(2)}) async-start(), calls=%async_computation.5 | async-start | bytes 2228224 | tf_op jit(solution)/shard_map/all_gather | solution.py:53
  26.5 10.1 %all-to-all-start = ((bf16[64,2,2048]{2,0,1:T(8,128)(2,1)}), bf16[64,2,2048]{2,0,1:T(8,128)(2,1)S(1)}, u32[]{:S(2)}, u32[]{:S(2)}) async-start(bf16[64,2,2048]{2,0,1:T(8,128)(2,1)} %bitcast.98), calls=%async_computation | async-start | bytes 1048576 | tf_op jit(solution)/shard_map/all_to_all | solution.py:31
  105.0 1.7 %copy-start = (bf16[2048,4,128]{0,2,1:T(8,128)(2,1)S(1)}, bf16[2048,4,128]{0,2,1:T(8,128)(2,1)}, u32[]{:S(2)}) copy-start(bf16[2048,4,128]{0,2,1:T(8,128)(2,1)} %get-tuple-element.98) | copy-start | bytes 6291460 | tf_op jit(solution)/shard_map/cond
  114.1 1.7 %copy-start.1 = (bf16[2048,4,128]{0,2,1:T(8,128)(2,1)S(1)}, bf16[2048,4,128]{0,2,1:T(8,128)(2,1)}, u32[]{:S(2)}) copy-start(bf16[2048,4,128]{0,2,1:T(8,128)(2,1)} %get-tuple-element.104) | copy-start | bytes 6291460 | tf_op jit(solution)/shard_map/cond
Sparse Core Ops, SparseCore 0:
  16.2 42.0 all-gather.2
  60.5 40.1 all-gather.4
where the time goes:
time: 144 us; the launch traced here: 143 us
  waiting for transfers between devices  64.6 us (45%)
  blocking collectives  27.2 us (19%)
  local copies, waits for them, and re-layouts  18.5 us (13%)
  between operations  14.8 us (10%)
  matrix products  7.21 us (5%)
  other arithmetic  6.63 us (5%)
  starting transfers between devices  3.53 us (2%)
    all_gather x1, waiting for transfers between devices, on_device(): value_piece = lax.all_gather(v_local, 'seq', axis=0, tiled=True)  39.4 us
    all_gather x1, waiting for transfers between devices, on_device(): key_piece = lax.all_gather(k_local, 'seq', axis=0, tiled=True)  21.2 us
    all_to_all x1, blocking collectives, on_device(): lax.all_to_all(combined, 'head', split_axis=0, concat_axis=1, tiled=True)  11.1 us
    all_to_all x1, blocking collectives, on_device(): lax.all_to_all(keys, 'head', split_axis=1, concat_axis=0, tiled=True)  8.64 us
    all_to_all x1, blocking collectives, on_device(): lax.all_to_all(values, 'head', split_axis=1, concat_axis=0, tiled=True)  7.52 us
    reduce_sum x2, other arithmetic, update_state(): total = jnp.sum(weight, axis=-1)  5.08 us
    all_to_all x1, waiting for transfers between devices, on_device(): lax.all_to_all(queries, 'head', split_axis=1, concat_axis=0, tiled=True)  3.99 us
    all_gather x1, local copies, waits for them, and re-layouts, on_device(): value_piece = lax.all_gather(v_local, 'seq', axis=0, tiled=True)  3.95 us
  transfers between devices with their start and end apart: 3, of which 3 were waited for; matrix products, arithmetic and copies ran while one was open for 5% of the time, Pallas kernels for 0%

commit v1 on v0

--- a/solution.py
+++ b/solution.py
@@ -49,7 +49,12 @@
         jnp.zeros((2, half, kv_local, group, HEAD_DIM), jnp.float32),
     )
     start = jnp.int32(0)
-    key_piece = lax.all_gather(k_local, "seq", axis=0, tiled=True)
+    ring = [k_local]
+    for hop in range(15):
+        ring.append(lax.ppermute(ring[-1], "seq", [(dev, (dev + 1) % 16) for dev in range(16)]))
+    key_piece = jnp.roll(
+        jnp.concatenate(ring[::-1], axis=0), (lax.axis_index("seq") + 1) * ring[0].shape[0], axis=0
+    )
     value_piece = lax.all_gather(v_local, "seq", axis=0, tiled=True)
     rows = key_piece.shape[0]
     key_piece = key_piece.reshape(rows, kv_local, HEAD_DIM)

time: 144 us -> 198 us (1.38)
  waiting for transfers between devices: 64.6 us -> 120 us
  blocking collectives: 27.2 us -> 19.6 us
  starting transfers between devices: 3.53 us -> 7 us
  local copies, waits for them, and re-layouts: 18.5 us -> 20.9 us
    ppermute x0 -> x15, waiting for transfers between devices: none -> 97.3 us  [on_device(): lax.ppermute(ring[-1], 'seq', [(dev, (dev + 1) % 16) for dev in range(16)])]
    all_gather x1 -> x0, waiting for transfers between devices: 21.2 us -> none  [on_device(): key_piece = lax.all_gather(k_local, 'seq', axis=0, tiled=True)]
    all_gather x1, waiting for transfers between devices: 39.4 us -> 19.6 us  [on_device(): value_piece = lax.all_gather(v_local, 'seq', axis=0, tiled=True)]
    all_to_all x1 -> x0, blocking collectives: 7.52 us -> none  [on_device(): lax.all_to_all(values, 'head', split_axis=1, concat_axis=0, tiled=True)]
    dynamic_slice x0 -> x2, local copies, waits for them, and re-layouts: none -> 4.4 us  [on_device(): jnp.roll(jnp.concatenate(ring[::-1], axis=0), (lax.axis_index('seq') + 1)...]
    all_to_all x1, waiting for transfers between devices: 3.99 us -> 0.01 us  [on_device(): lax.all_to_all(queries, 'head', split_axis=1, concat_axis=0, tiled=True)]
    all_to_all x0 -> x1, starting transfers between devices: none -> 3.38 us  [on_device(): lax.all_to_all(values, 'head', split_axis=1, concat_axis=0, tiled=True)]
    all_to_all x0 -> x1, waiting for transfers between devices: none -> 3.17 us  [on_device(): lax.all_to_all(values, 'head', split_axis=1, concat_axis=0, tiled=True)]
  transfers between devices with their start and end apart: 3 -> 18, of which waited for: 3 -> 16; matrix products, arithmetic and copies ran while one was open for 5% -> 5% of each run, Pallas kernels for 0% -> 0%
where the time goes in v1:
time: 198 us; the launch traced here: 197 us
  waiting for transfers between devices  120 us (61%)
  local copies, waits for them, and re-layouts  20.9 us (11%)
  blocking collectives  19.6 us (10%)
  between operations  15.1 us (8%)
  matrix products  7.21 us (4%)
  starting transfers between devices  7 us (4%)
  other arithmetic  6.63 us (3%)
    ppermute x15, waiting for transfers between devices, on_device(): lax.ppermute(ring[-1], 'seq', [(dev, (dev + 1) % 16) for dev in range(16)])  97.3 us
    all_gather x1, waiting for transfers between devices, on_device(): value_piece = lax.all_gather(v_local, 'seq', axis=0, tiled=True)  19.6 us
    all_to_all x1, blocking collectives, on_device(): lax.all_to_all(combined, 'head', split_axis=0, concat_axis=1, tiled=True)  11.1 us
    all_to_all x1, blocking collectives, on_device(): lax.all_to_all(keys, 'head', split_axis=1, concat_axis=0, tiled=True)  8.54 us
    reduce_sum x2, other arithmetic, update_state(): total = jnp.sum(weight, axis=-1)  5.08 us
    dynamic_slice x2, local copies, waits for them, and re-layouts, on_device(): jnp.roll(jnp.concatenate(ring[::-1], axis=0), (lax.axis_index('seq') + 1)...  4.4 us
    all_gather x1, local copies, waits for them, and re-layouts, on_device(): value_piece = lax.all_gather(v_local, 'seq', axis=0, tiled=True)  3.97 us
  transfers between devices with their start and end apart: 18, of which 16 were waited for; matrix products, arithmetic and copies ran while one was open for 5% of the time, Pallas kernels for 0%

profile of v1, /device:TPU:0, one launch (start us, length us, event | category | flops | bytes accessed | tf_op | source)
XLA Modules:
  0.0 196.9 jit_solution(14367997923555917838)
XLA Ops:
  7.5 8.5 %all_to_all.73 = bf16[64,2,512]{2,0,1:T(8,128)(2,1)S(1)} all-to-all(bf16[64,2,512]{2,0,1:T(8,128)(2,1)S(1)} %bitcast.113), channel_id=1, replica_groups=mesh['head'=2,'seq'=16] {'head'}, dimensions={1} | all-to-all | bytes 262144 | tf_op jit(solution)/shard_map/all_to_all | solution.py:32
  16.0 7.1 %collective-permute-done = bf16[128,512]{1,0:T(8,128)(2,1)S(1)} collective-permute-done((bf16[128,512]{1,0:T(8,128)(2,1)S(1)}, bf16[128,512]{1,0:T(8,128)(2,1)S(1)}, u32[]{:S(2)}, u32[]{:S(2)}) %collective-permute-start) | collective-permute-done | bytes 131104 | tf_op jit(solution)/shard_map/ppermute | solution.py:54
  23.1 7.1 %collective-permute-done.1 = bf16[128,512]{1,0:T(8,128)(2,1)S(1)} collective-permute-done((bf16[128,512]{1,0:T(8,128)(2,1)S(1)}, bf16[128,512]{1,0:T(8,128)(2,1)S(1)}, u32[]{:S(2)}, u32[]{:S(2)}) %collective-permute-start.1) | collective-permute-done | bytes 131104 | tf_op jit(solution)/shard_map/ppermute | solution.py:54
  30.2 7.1 %collective-permute-done.2 = bf16[128,512]{1,0:T(8,128)(2,1)S(1)} collective-permute-done((bf16[128,512]{1,0:T(8,128)(2,1)S(1)}, bf16[128,512]{1,0:T(8,128)(2,1)S(1)}, u32[]{:S(2)}, u32[]{:S(2)}) %collective-permute-start.2) | collective-permute-done | bytes 131104 | tf_op jit(solution)/shard_map/ppermute | solution.py:54
  37.3 7.1 %collective-permute-done.3 = bf16[128,512]{1,0:T(8,128)(2,1)S(1)} collective-permute-done((bf16[128,512]{1,0:T(8,128)(2,1)S(1)}, bf16[128,512]{1,0:T(8,128)(2,1)S(1)}, u32[]{:S(2)}, u32[]{:S(2)}) %collective-permute-start.3) | collective-permute-done | bytes 131104 | tf_op jit(solution)/shard_map/ppermute | solution.py:54
  44.4 7.1 %collective-permute-done.4 = bf16[128,512]{1,0:T(8,128)(2,1)S(1)} collective-permute-done((bf16[128,512]{1,0:T(8,128)(2,1)S(1)}, bf16[128,512]{1,0:T(8,128)(2,1)S(1)}, u32[]{:S(2)}, u32[]{:S(2)}) %collective-permute-start.4) | collective-permute-done | bytes 131104 | tf_op jit(solution)/shard_map/ppermute | solution.py:54
  51.4 7.1 %collective-permute-done.5 = bf16[128,512]{1,0:T(8,128)(2,1)S(1)} collective-permute-done((bf16[128,512]{1,0:T(8,128)(2,1)S(1)}, bf16[128,512]{1,0:T(8,128)(2,1)S(1)}, u32[]{:S(2)}, u32[]{:S(2)}) %collective-permute-start.5) | collective-permute-done | bytes 131104 | tf_op jit(solution)/shard_map/ppermute | solution.py:54
  58.5 7.1 %collective-permute-done.6 = bf16[128,512]{1,0:T(8,128)(2,1)S(1)} collective-permute-done((bf16[128,512]{1,0:T(8,128)(2,1)S(1)}, bf16[128,512]{1,0:T(8,128)(2,1)S(1)}, u32[]{:S(2)}, u32[]{:S(2)}) %collective-permute-start.6) | collective-permute-done | bytes 131104 | tf_op jit(solution)/shard_map/ppermute | solution.py:54
  65.6 7.1 %collective-permute-done.7 = bf16[128,512]{1,0:T(8,128)(2,1)S(1)} collective-permute-done((bf16[128,512]{1,0:T(8,128)(2,1)S(1)}, bf16[128,512]{1,0:T(8,128)(2,1)S(1)}, u32[]{:S(2)}, u32[]{:S(2)}) %collective-permute-start.7) | collective-permute-done | bytes 131104 | tf_op jit(solution)/shard_map/ppermute | solution.py:54
  72.7 7.1 %collective-permute-done.8 = bf16[128,512]{1,0:T(8,128)(2,1)S(1)} collective-permute-done((bf16[128,512]{1,0:T(8,128)(2,1)S(1)}, bf16[128,512]{1,0:T(8,128)(2,1)S(1)}, u32[]{:S(2)}, u32[]{:S(2)}) %collective-permute-start.8) | collective-permute-done | bytes 131104 | tf_op jit(solution)/shard_map/ppermute | solution.py:54
  79.8 7.1 %collective-permute-done.9 = bf16[128,512]{1,0:T(8,128)(2,1)S(1)} collective-permute-done((bf16[128,512]{1,0:T(8,128)(2,1)S(1)}, bf16[128,512]{1,0:T(8,128)(2,1)S(1)}, u32[]{:S(2)}, u32[]{:S(2)}) %collective-permute-start.9) | collective-permute-done | bytes 131104 | tf_op jit(solution)/shard_map/ppermute | solution.py:54
  86.9 7.1 %collective-permute-done.10 = bf16[128,512]{1,0:T(8,128)(2,1)S(1)} collective-permute-done((bf16[128,512]{1,0:T(8,128)(2,1)S(1)}, bf16[128,512]{1,0:T(8,128)(2,1)S(1)}, u32[]{:S(2)}, u32[]{:S(2)}) %collective-permute-start.10) | collective-permute-done | bytes 131104 | tf_op jit(solution)/shard_map/ppermute | solution.py:54
  95.5 3.4 %all-to-all-start.2 = ((bf16[64,2,512]{2,0,1:T(8,128)(2,1)}), bf16[64,2,512]{2,0,1:T(8,128)(2,1)S(1)}, u32[]{:S(2)}, u32[]{:S(2)}) async-start(bf16[64,2,512]{2,0,1:T(8,128)(2,1)} %bitcast.99), calls=%async_computation.2 | async-start | bytes 262144 | tf_op jit(solution)/shard_map/all_to_all | solution.py:33
  100.8 3.2 %all-to-all-done.2 = bf16[64,2,512]{2,0,1:T(8,128)(2,1)S(1)} async-done(((bf16[64,2,512]{2,0,1:T(8,128)(2,1)}), bf16[64,2,512]{2,0,1:T(8,128)(2,1)S(1)}, u32[]{:S(2)}, u32[]{:S(2)}) %all-to-all-start.2) | async-done | bytes 131104 | tf_op jit(solution)/shard_map/all_to_all | solution.py:33
  104.0 3.5 %all-to-all-start = ((bf16[64,2,2048]{2,0,1:T(8,128)(2,1)}), bf16[64,2,2048]{2,0,1:T(8,128)(2,1)S(1)}, u32[]{:S(2)}, u32[]{:S(2)}) async-start(bf16[64,2,2048]{2,0,1:T(8,128)(2,1)} %bitcast.98), calls=%async_computation | async-start | bytes 1048576 | tf_op jit(solution)/shard_map/all_to_all | solution.py:31
  110.2 4.5 %collective-permute-done.12 = bf16[128,512]{1,0:T(8,128)(2,1)S(1)} collective-permute-done((bf16[128,512]{1,0:T(8,128)(2,1)S(1)}, bf16[128,512]{1,0:T(8,128)(2,1)S(1)}, u32[]{:S(2)}, u32[]{:S(2)}) %collective-permute-start.12) | collective-permute-done | bytes 131104 | tf_op jit(solution)/shard_map/ppermute | solution.py:54
  114.9 6.9 %collective-permute-done.13 = bf16[128,512]{1,0:T(8,128)(2,1)S(1)} collective-permute-done((bf16[128,512]{1,0:T(8,128)(2,1)S(1)}, bf16[128,512]{1,0:T(8,128)(2,1)S(1)}, u32[]{:S(2)}, u32[]{:S(2)}) %collective-permute-start.13) | collective-permute-done | bytes 131104 | tf_op jit(solution)/shard_map/ppermute | solution.py:54
  122.2 8.0 %collective-permute-done.14 = bf16[128,512]{1,0:T(8,128)(2,1)S(1)} collective-permute-done((bf16[128,512]{1,0:T(8,128)(2,1)S(1)}, bf16[128,512]{1,0:T(8,128)(2,1)S(1)}, u32[]{:S(2)}, u32[]{:S(2)}) %collective-permute-start.14) | collective-permute-done | bytes 131104 | tf_op jit(solution)/shard_map/ppermute | solution.py:54
  132.2 2.9 %copy.49 = bf16[2048,512]{0,1:T(8,128)(2,1)S(1)} copy(bf16[2048,512]{1,0:T(8,128)(2,1)} %constant_dynamic-slice_fusion) | data formatting | bytes 4194304 | tf_op jit(solution)/shard_map/jit(_roll_dynamic)/dynamic_slice | solution.py:55
  135.1 19.6 %all-gather.2.cloned.1.call-done = bf16[2048,512]{1,0:T(8,128)(2,1)} async-done(((bf16[128,512]{1,0:T(8,128)(2,1)}), bf16[2048,512]{1,0:T(8,128)(2,1)}) %all-gather.2.cloned.1.call-update) | async-done | bytes 2097168 | tf_op jit(solution)/shard_map/all_gather | solution.py:58
  154.8 4.0 %copy.51 = bf16[2048,512]{0,1:T(8,128)(2,1)} copy(bf16[2048,512]{1,0:T(8,128)(2,1)} %all-gather.2.cloned.1.call-done) | data formatting | bytes 4194304 | tf_op jit(solution)/shard_map/all_gather | solution.py:58
  158.8 8.9 %conditional.2 = (f32[1,64,4,4]{1,3,2,0:T(4,128)S(1)}, f32[1,64,2048]{2,1,0:T(8,128)S(1)}) conditional(s32[]{:T(128)} %bitcast.12, () %tuple.29, (s32[2048]{0:T(1024)S(1)}, s32[]{:T(128)}, s32[64]{0:T(128)S(1)}, bf16[2,64,4,4,128]{4,3,2,1,0:T(4,128)(2,1)S(1)}, bf16[2048,4,128]{0,2,1:T(8,128)(2,1)S(1)}, ...), branch_computations={%region_0.1_spmd, %region_1.4_spmd} | conditional | flops 1101134848 | bytes 42238768 | solution.py:76
  167.7 8.0 %conditional.3 = (f32[1,64,4,4]{1,3,2,0:T(4,128)S(1)}, f32[1,64,2048]{2,1,0:T(8,128)}) conditional(s32[]{:T(128)} %bitcast.20, () %tuple.31, (s32[2048]{0:T(1024)S(1)}, s32[]{:T(128)}, s32[64]{0:T(128)S(1)}, bf16[2,64,4,4,128]{4,3,2,1,0:T(4,128)(2,1)S(1)}, bf16[2048,4,128]{0,2,1:T(8,128)(2,1)S(1)}, /*index=5*/bf16[2048,4,128]{0,2,1:T(8,128)(2,1)}) %tuple.54), branch_computations={%region_4.5_spmd, %region_5.8_spmd} | conditional | flops 1101134848 | bytes 42238768 | solution.py:76
  178.2 11.1 %all_to_all.74 = bf16[2,64,2048]{2,1,0:T(8,128)(2,1)S(1)} all-to-all(bf16[2,64,2048]{2,1,0:T(8,128)(2,1)S(1)} %bitcast.106), channel_id=1, replica_groups=mesh['head'=2,'seq'=16] {'head'}, dimensions={0} | all-to-all | bytes 1048576 | tf_op jit(solution)/shard_map/all_to_all | solution.py:82
  (100 shorter events, 28.0 us)
Async XLA Ops:
  16.0 7.1 %collective-permute-start = (bf16[128,512]{1,0:T(8,128)(2,1)S(1)}, bf16[128,512]{1,0:T(8,128)(2,1)S(1)}, u32[]{:S(2)}, u32[]{:S(2)}) collective-permute-start(bf16[128,512]{1,0:T(8,128)(2,1)S(1)} %bitcast.108), channel_id=1, source_target_pairs={{0,1},{1,2},{2,3},{3,4},{4,5},{5,6},{6,7},{7,8},{8,9},{9,10},{10,1... | collective-permute-start | bytes 393224 | tf_op jit(solution)/shard_map/ppermute | solution.py:54
  23.1 7.1 %collective-permute-start.1 = (bf16[128,512]{1,0:T(8,128)(2,1)S(1)}, bf16[128,512]{1,0:T(8,128)(2,1)S(1)}, u32[]{:S(2)}, u32[]{:S(2)}) collective-permute-start(bf16[128,512]{1,0:T(8,128)(2,1)S(1)} %collective-permute-done), channel_id=1, source_target_pairs={{0,1},{1,2},{2,3},{3,4},{4,5},{5,6},{6,7},{7,8},{8,9},{9,10},{10,1... | collective-permute-start | bytes 393224 | tf_op jit(solution)/shard_map/ppermute | solution.py:54
  30.2 7.1 %collective-permute-start.2 = (bf16[128,512]{1,0:T(8,128)(2,1)S(1)}, bf16[128,512]{1,0:T(8,128)(2,1)S(1)}, u32[]{:S(2)}, u32[]{:S(2)}) collective-permute-start(bf16[128,512]{1,0:T(8,128)(2,1)S(1)} %collective-permute-done.1), channel_id=1, source_target_pairs={{0,1},{1,2},{2,3},{3,4},{4,5},{5,6},{6,7},{7,8},{8,9},{9,10},{10,1... | collective-permute-start | bytes 393224 | tf_op jit(solution)/shard_map/ppermute | solution.py:54
  37.3 7.1 %collective-permute-start.3 = (bf16[128,512]{1,0:T(8,128)(2,1)S(1)}, bf16[128,512]{1,0:T(8,128)(2,1)S(1)}, u32[]{:S(2)}, u32[]{:S(2)}) collective-permute-start(bf16[128,512]{1,0:T(8,128)(2,1)S(1)} %collective-permute-done.2), channel_id=1, source_target_pairs={{0,1},{1,2},{2,3},{3,4},{4,5},{5,6},{6,7},{7,8},{8,9},{9,10},{10,1... | collective-permute-start | bytes 393224 | tf_op jit(solution)/shard_map/ppermute | solution.py:54
  44.3 7.1 %collective-permute-start.4 = (bf16[128,512]{1,0:T(8,128)(2,1)S(1)}, bf16[128,512]{1,0:T(8,128)(2,1)S(1)}, u32[]{:S(2)}, u32[]{:S(2)}) collective-permute-start(bf16[128,512]{1,0:T(8,128)(2,1)S(1)} %collective-permute-done.3), channel_id=1, source_target_pairs={{0,1},{1,2},{2,3},{3,4},{4,5},{5,6},{6,7},{7,8},{8,9},{9,10},{10,1... | collective-permute-start | bytes 393224 | tf_op jit(solution)/shard_map/ppermute | solution.py:54
  51.4 7.1 %collective-permute-start.5 = (bf16[128,512]{1,0:T(8,128)(2,1)S(1)}, bf16[128,512]{1,0:T(8,128)(2,1)S(1)}, u32[]{:S(2)}, u32[]{:S(2)}) collective-permute-start(bf16[128,512]{1,0:T(8,128)(2,1)S(1)} %collective-permute-done.4), channel_id=1, source_target_pairs={{0,1},{1,2},{2,3},{3,4},{4,5},{5,6},{6,7},{7,8},{8,9},{9,10},{10,1... | collective-permute-start | bytes 393224 | tf_op jit(solution)/shard_map/ppermute | solution.py:54
  58.5 7.1 %collective-permute-start.6 = (bf16[128,512]{1,0:T(8,128)(2,1)S(1)}, bf16[128,512]{1,0:T(8,128)(2,1)S(1)}, u32[]{:S(2)}, u32[]{:S(2)}) collective-permute-start(bf16[128,512]{1,0:T(8,128)(2,1)S(1)} %collective-permute-done.5), channel_id=1, source_target_pairs={{0,1},{1,2},{2,3},{3,4},{4,5},{5,6},{6,7},{7,8},{8,9},{9,10},{10,1... | collective-permute-start | bytes 393224 | tf_op jit(solution)/shard_map/ppermute | solution.py:54
  65.6 7.1 %collective-permute-start.7 = (bf16[128,512]{1,0:T(8,128)(2,1)S(1)}, bf16[128,512]{1,0:T(8,128)(2,1)S(1)}, u32[]{:S(2)}, u32[]{:S(2)}) collective-permute-start(bf16[128,512]{1,0:T(8,128)(2,1)S(1)} %collective-permute-done.6), channel_id=1, source_target_pairs={{0,1},{1,2},{2,3},{3,4},{4,5},{5,6},{6,7},{7,8},{8,9},{9,10},{10,1... | collective-permute-start | bytes 393224 | tf_op jit(solution)/shard_map/ppermute | solution.py:54
  72.7 7.1 %collective-permute-start.8 = (bf16[128,512]{1,0:T(8,128)(2,1)S(1)}, bf16[128,512]{1,0:T(8,128)(2,1)S(1)}, u32[]{:S(2)}, u32[]{:S(2)}) collective-permute-start(bf16[128,512]{1,0:T(8,128)(2,1)S(1)} %collective-permute-done.7), channel_id=1, source_target_pairs={{0,1},{1,2},{2,3},{3,4},{4,5},{5,6},{6,7},{7,8},{8,9},{9,10},{10,1... | collective-permute-start | bytes 393224 | tf_op jit(solution)/shard_map/ppermute | solution.py:54
  79.8 7.1 %collective-permute-start.9 = (bf16[128,512]{1,0:T(8,128)(2,1)S(1)}, bf16[128,512]{1,0:T(8,128)(2,1)S(1)}, u32[]{:S(2)}, u32[]{:S(2)}) collective-permute-start(bf16[128,512]{1,0:T(8,128)(2,1)S(1)} %collective-permute-done.8), channel_id=1, source_target_pairs={{0,1},{1,2},{2,3},{3,4},{4,5},{5,6},{6,7},{7,8},{8,9},{9,10},{10,1... | collective-permute-start | bytes 393224 | tf_op jit(solution)/shard_map/ppermute | solution.py:54
  86.9 7.1 %collective-permute-start.10 = (bf16[128,512]{1,0:T(8,128)(2,1)S(1)}, bf16[128,512]{1,0:T(8,128)(2,1)S(1)}, u32[]{:S(2)}, u32[]{:S(2)}) collective-permute-start(bf16[128,512]{1,0:T(8,128)(2,1)S(1)} %collective-permute-done.9), channel_id=1, source_target_pairs={{0,1},{1,2},{2,3},{3,4},{4,5},{5,6},{6,7},{7,8},{8,9},{9,10},{10,1... | collective-permute-start | bytes 393224 | tf_op jit(solution)/shard_map/ppermute | solution.py:54
  94.0 13.6 %collective-permute-start.11 = (bf16[128,512]{1,0:T(8,128)(2,1)S(1)}, bf16[128,512]{1,0:T(8,128)(2,1)S(1)}, u32[]{:S(2)}, u32[]{:S(2)}) collective-permute-start(bf16[128,512]{1,0:T(8,128)(2,1)S(1)} %collective-permute-done.10), channel_id=1, source_target_pairs={{0,1},{1,2},{2,3},{3,4},{4,5},{5,6},{6,7},{7,8},{8,9},{9,10},{10,1... | collective-permute-start | bytes 393224 | tf_op jit(solution)/shard_map/ppermute | solution.py:54
  95.5 8.4 %all-to-all-start.2 = ((bf16[64,2,512]{2,0,1:T(8,128)(2,1)}), bf16[64,2,512]{2,0,1:T(8,128)(2,1)S(1)}, u32[]{:S(2)}, u32[]{:S(2)}) async-start(bf16[64,2,512]{2,0,1:T(8,128)(2,1)} %bitcast.99), calls=%async_computation.2 | async-start | bytes 262144 | tf_op jit(solution)/shard_map/all_to_all | solution.py:33
  104.0 6.1 %copy-start.2 = (bf16[64,2,512]{2,0,1:T(8,128)(2,1)}, bf16[64,2,512]{2,0,1:T(8,128)(2,1)S(1)}, u32[]{:S(2)}) copy-start(bf16[64,2,512]{2,0,1:T(8,128)(2,1)S(1)} %all-to-all-done.2) | copy-start | bytes 393220
  104.0 10.7 %all-to-all-start = ((bf16[64,2,2048]{2,0,1:T(8,128)(2,1)}), bf16[64,2,2048]{2,0,1:T(8,128)(2,1)S(1)}, u32[]{:S(2)}, u32[]{:S(2)}) async-start(bf16[64,2,2048]{2,0,1:T(8,128)(2,1)} %bitcast.98), calls=%async_computation | async-start | bytes 1048576 | tf_op jit(solution)/shard_map/all_to_all | solution.py:31
  107.5 47.3 %all-gather.2.cloned.1.call-start = ((), (), s32[]{:S(2)}) async-start(), calls=%async_computation.4 | async-start | bytes 2228224 | tf_op jit(solution)/shard_map/all_gather | solution.py:58
  107.5 7.1 %collective-permute-start.12 = (bf16[128,512]{1,0:T(8,128)(2,1)S(1)}, bf16[128,512]{1,0:T(8,128)(2,1)S(1)}, u32[]{:S(2)}, u32[]{:S(2)}) collective-permute-start(bf16[128,512]{1,0:T(8,128)(2,1)S(1)} %collective-permute-done.11), channel_id=1, source_target_pairs={{0,1},{1,2},{2,3},{3,4},{4,5},{5,6},{6,7},{7,8},{8,9},{9,10},{10,1... | collective-permute-start | bytes 393224 | tf_op jit(solution)/shard_map/ppermute | solution.py:54
  114.7 7.1 %collective-permute-start.13 = (bf16[128,512]{1,0:T(8,128)(2,1)S(1)}, bf16[128,512]{1,0:T(8,128)(2,1)S(1)}, u32[]{:S(2)}, u32[]{:S(2)}) collective-permute-start(bf16[128,512]{1,0:T(8,128)(2,1)S(1)} %collective-permute-done.12), channel_id=1, source_target_pairs={{0,1},{1,2},{2,3},{3,4},{4,5},{5,6},{6,7},{7,8},{8,9},{9,10},{10,1... | collective-permute-start | bytes 393224 | tf_op jit(solution)/shard_map/ppermute | solution.py:54
  121.8 8.3 %collective-permute-start.14 = (bf16[128,512]{1,0:T(8,128)(2,1)S(1)}, bf16[128,512]{1,0:T(8,128)(2,1)S(1)}, u32[]{:S(2)}, u32[]{:S(2)}) collective-permute-start(bf16[128,512]{1,0:T(8,128)(2,1)S(1)} %collective-permute-done.13), channel_id=1, source_target_pairs={{0,1},{1,2},{2,3},{3,4},{4,5},{5,6},{6,7},{7,8},{8,9},{9,10},{10,1... | collective-permute-start | bytes 393224 | tf_op jit(solution)/shard_map/ppermute | solution.py:54
  159.1 1.7 copy-start
  168.2 1.7 copy-start.1
Sparse Core Ops, SparseCore 0:
  110.5 44.2 all-gather.1
